TPU v7x, 32 devices: a whole 2x2x4 slice. The times are simulated.
32 devices in a mesh: cp: 8 (over y, x, core), tp: 4 (over z).
Axes of the slice: x: 2, y: 2, z: 4, core: 2. Of those that a mesh axis runs over, the one named last changes fastest.
Arguments:
- hidden: bfloat16 [2048, 4096], P('cp', 'tp'), may hold values from -120 to 120
- query_weight: bfloat16 [4096, 4096], P(None, 'tp'), may hold values from -0.1875 to 0.1875
- key_matrix: bfloat16 [4096, 512], P(None, 'tp'), may hold values from -0.09375 to 0.09375
- value_matrix: bfloat16 [4096, 512], P(None, 'tp'), may hold values from -0.09375 to 0.09375
- output_weight: bfloat16 [4096, 4096], P('tp'), may hold values from -0.1875 to 0.1875
- document_bounds: int32 [9], replicated, may hold values from 0 to 2048, as said below
- block_owner: int32 [16], replicated, may hold values from 0 to 7, as said below
Outputs:
- attended: bfloat16 [2048, 4096], P('cp', 'tp')
Inputs may be any that keep to these rules, and one draw needn't show every extreme that they name: document_bounds[0] = 0, document_bounds[8] = 2048, strictly rising; document i holds the tokens from document_bounds[i] to document_bounds[i + 1] - 1. `block_owner`: every index of cp is named by exactly 2 blocks.
All inputs are finite; a program needn't handle non-finite values.
Results may differ from a plain program's by a relative error of at most 0.012.
The roundings to bfloat16 on the way count: a program that leaves them out, or rounds other values in their place, can miss the bound.
Values may be sent and summed in bfloat16 or wider, within the bound.
A program may use at most 128 MiB of HBM per device.

v0:
```python
import math
import jax
import jax.numpy as jnp
from jax import lax
from jax.sharding import PartitionSpec as P

HEAD_WIDTH = 128
BLOCK = 128
rope_theta = 500000.0
rope_factor = 8.0
rope_context = 8192.0
masked_score = -1e30


def rope_inverse(head_size):
    halves = jnp.arange(head_size // 2, dtype=jnp.float32)
    inverse = 1.0 / rope_theta ** (2.0 * halves / head_size)
    wavelength = 2.0 * math.pi / inverse
    smooth = (rope_context / wavelength - 1.0) / 3.0
    blended = (1.0 - smooth) * inverse / rope_factor + smooth * inverse
    longer = jnp.where(wavelength > rope_context, inverse / rope_factor, blended)
    return jnp.where(wavelength < rope_context / 4.0, inverse, longer)


def document_of(tokens, bounds):
    inner_bounds = bounds[1:-1]
    return jnp.sum((tokens[:, None] >= inner_bounds[None, :]).astype(jnp.int32), axis=1)


def position_of(tokens, bounds):
    starts = bounds[:-1]
    document_start = jnp.max(
        jnp.where(starts[None, :] <= tokens[:, None], starts[None, :], 0), axis=1
    )
    return tokens - document_start


def rotate(raw_rows, tokens, bounds, head_size):
    row_count = raw_rows.shape[0]
    head_count = raw_rows.shape[1] // head_size
    angles = (
        position_of(tokens, bounds).astype(jnp.float32)[:, None] * rope_inverse(head_size)[None, :]
    )
    cosine = jnp.cos(angles)[:, None, :]
    sine_table = jnp.sin(angles)[:, None, :]
    heads_view = raw_rows.reshape(row_count, head_count, head_size)
    front_half = heads_view[:, :, : head_size // 2]
    back_half = heads_view[:, :, head_size // 2 :]
    turned = jnp.concatenate(
        [
            front_half * cosine - back_half * sine_table,
            back_half * cosine + front_half * sine_table,
        ],
        axis=2,
    )
    return turned.reshape(row_count, head_count * head_size).astype(jnp.bfloat16)


def owner_order(block_owner, per_device):
    block_count = block_owner.shape[0]
    blocks = jnp.arange(block_count, dtype=jnp.int32)
    same_owner = block_owner[:, None] == block_owner[None, :]
    earlier = blocks[None, :] < blocks[:, None]
    owner_rank = jnp.sum((same_owner & earlier).astype(jnp.int32), axis=1)
    target = block_owner * per_device + owner_rank
    return jnp.sum(jnp.where(target[None, :] == blocks[:, None], blocks[None, :], 0), axis=1)


def relayout(local_rows, block_order):
    cp_size = lax.axis_size("cp")
    row_count, row_width = local_rows.shape
    per_device = row_count // BLOCK
    portion = BLOCK // cp_size
    pieces = local_rows.reshape(per_device, cp_size, portion * row_width)
    spread = lax.all_to_all(pieces, "cp", split_axis=1, concat_axis=0, tiled=True)
    spread = spread.reshape(per_device * cp_size, portion * row_width)
    wanted = block_order.reshape(cp_size, per_device).T.reshape(-1)
    outgoing = jnp.take(spread, wanted, axis=0).reshape(per_device, cp_size, portion * row_width)
    arrived = lax.all_to_all(outgoing, "cp", split_axis=1, concat_axis=1, tiled=True)
    return arrived.reshape(row_count, row_width)


def project(local_rows, query_weight, key_matrix, value_matrix):
    weight_list = (query_weight, key_matrix, value_matrix)
    portion = lax.all_gather(local_rows, "tp", axis=1, tiled=True)
    return tuple(
        (jnp.dot(portion, weight, preferred_element_type=jnp.float32) for weight in weight_list)
    )


def attend(queries, query_tokens, key_rows, value_rows, key_tokens, bounds, head_size, kv_heads):
    row_count = queries.shape[0]
    query_group_width = queries.shape[1] // (kv_heads * head_size)
    grouped = queries.reshape(row_count, kv_heads, query_group_width, head_size).transpose(
        1, 2, 0, 3
    )
    grouped = grouped.reshape(kv_heads, query_group_width * row_count, head_size)
    query_documents = document_of(query_tokens, bounds)
    score_scale = 1.0 / math.sqrt(head_size)

    def update(flash_state, key_block, value_block, token_block):
        block_rows = key_block.shape[0]
        key_documents = document_of(token_block, bounds)
        allowed = (query_documents[:, None] == key_documents[None, :]) & (
            token_block[None, :] <= query_tokens[:, None]
        )
        running_max, running_sum, running_out = flash_state
        per_head_keys = key_block.reshape(block_rows, kv_heads, head_size).transpose(1, 0, 2)
        per_head_values = value_block.reshape(block_rows, kv_heads, head_size).transpose(1, 0, 2)
        scores = (
            jnp.einsum("khd,ksd->khs", grouped, per_head_keys, preferred_element_type=jnp.float32)
            * score_scale
        )
        wide_mask = jnp.tile(allowed, (query_group_width, 1))[None, :, :]
        scores = jnp.where(wide_mask, scores, masked_score)
        new_max = jnp.maximum(running_max, jnp.max(scores, axis=2))
        weights = jnp.where(wide_mask, jnp.exp(scores - new_max[:, :, None]), 0.0)
        factor = jnp.exp(running_max - new_max)
        new_sum = running_sum * factor + jnp.sum(weights, axis=2)
        new_out = running_out * factor[:, :, None] + jnp.einsum(
            "khs,ksd->khd",
            weights.astype(jnp.bfloat16),
            per_head_values,
            preferred_element_type=jnp.float32,
        )
        return (new_max, new_sum, new_out)

    initial = (
        jnp.full((kv_heads, query_group_width * row_count), masked_score, jnp.float32),
        jnp.zeros((kv_heads, query_group_width * row_count), jnp.float32),
        jnp.zeros((kv_heads, query_group_width * row_count, head_size), jnp.float32),
    )
    key_part = lax.all_gather(key_rows, "cp", axis=0, tiled=True)
    value_part = lax.all_gather(value_rows, "cp", axis=0, tiled=True)
    token_part = lax.all_gather(key_tokens, "cp", axis=0, tiled=True)
    part_rows = key_part.shape[0]
    block_rows = math.gcd(part_rows, 512)

    def one_block(block_index, inner_state):
        first_row = block_index * block_rows
        return update(
            inner_state,
            lax.dynamic_slice_in_dim(key_part, first_row, block_rows, 0),
            lax.dynamic_slice_in_dim(value_part, first_row, block_rows, 0),
            lax.dynamic_slice_in_dim(token_part, first_row, block_rows, 0),
        )

    final_max, final_sum, final_out = lax.fori_loop(0, part_rows // block_rows, one_block, initial)
    normalized = final_out / final_sum[:, :, None]
    merged = normalized.reshape(kv_heads, query_group_width, row_count, head_size).transpose(
        2, 0, 1, 3
    )
    return merged.reshape(row_count, kv_heads * query_group_width * head_size).astype(jnp.bfloat16)


def output_rows(heads_out, output_weight):
    head_terms = jnp.dot(heads_out, output_weight, preferred_element_type=jnp.float32)
    return lax.psum_scatter(head_terms.astype(jnp.bfloat16), "tp", scatter_dimension=1, tiled=True)


def local(
    hidden, query_weight, key_matrix, value_matrix, output_weight, document_bounds, block_owner
):
    cp_index = lax.axis_index("cp")
    row_count = hidden.shape[0]
    per_device = row_count // BLOCK
    block_order = owner_order(block_owner, per_device)
    own_blocks = lax.dynamic_slice_in_dim(block_order, cp_index * per_device, per_device, 0)
    new_tokens = (
        own_blocks[:, None] * BLOCK + jnp.arange(BLOCK, dtype=jnp.int32)[None, :]
    ).reshape(-1)
    kv_heads = key_matrix.shape[1] // HEAD_WIDTH
    moved = relayout(hidden, block_order)
    query_raw, key_raw, value_raw = project(moved, query_weight, key_matrix, value_matrix)
    queries = rotate(query_raw, new_tokens, document_bounds, HEAD_WIDTH)
    key_rows = rotate(key_raw, new_tokens, document_bounds, HEAD_WIDTH)
    value_rows = value_raw.astype(jnp.bfloat16)
    heads_out = attend(
        queries, new_tokens, key_rows, value_rows, new_tokens, document_bounds, HEAD_WIDTH, kv_heads
    )
    return output_rows(heads_out, output_weight)


def solution(mesh):
    placed = (P("cp", "tp"), P(None, "tp"), P(None, "tp"), P(None, "tp"), P("tp", None), P(), P())
    return jax.shard_map(
        local, mesh=mesh, in_specs=placed, out_specs=P("cp", "tp"), check_vma=False
    )
```

profile of v0, /device:TPU:0, one launch (start us, length us, event | category | flops | bytes accessed | tf_op | source)
XLA Modules:
  0.0 201.7 jit_solution(1744247314047454510)
XLA Ops:
  6.5 1.4 reshape.365
  7.9 1.3 copy.37
  9.2 5.2 %all-to-all-start = ((bf16[2,8,16384]{2,0,1:T(2,128)(2,1)}), bf16[2,8,16384]{2,0,1:T(2,128)(2,1)S(1)}, u32[]{:S(2)}, u32[]{:S(2)}) async-start(bf16[2,8,16384]{2,0,1:T(2,128)(2,1)} %copy.37), calls=%async_computation | async-start | bytes 1048576 | tf_op jit(solution)/shard_map/all_to_all | solution.py:75
  14.5 0.9 convert_reduce_fusion.2
  15.4 0.7 multiply_add_fusion
  16.5 7.7 %all-to-all-done = bf16[2,8,16384]{2,0,1:T(2,128)(2,1)S(1)} async-done(((bf16[2,8,16384]{2,0,1:T(2,128)(2,1)}), bf16[2,8,16384]{2,0,1:T(2,128)(2,1)S(1)}, u32[]{:S(2)}, u32[]{:S(2)}) %all-to-all-start) | async-done | bytes 524320 | tf_op jit(solution)/shard_map/all_to_all | solution.py:75
  24.4 0.9 gather_fusion
  25.3 0.9 broadcast_select_fusion.2
  26.2 12.1 %all_to_all.20 = bf16[2,8,16384]{2,0,1:T(2,128)(2,1)S(1)} all-to-all(bf16[2,8,16384]{2,0,1:T(2,128)(2,1)S(1)} %broadcast_select_fusion.2), channel_id=1, replica_groups=mesh['cp'=8,'tp'=4] {'cp'}, dimensions={1} | all-to-all | bytes 1048576 | tf_op jit(solution)/shard_map/all_to_all | solution.py:79
  38.3 0.3 copy.40
  38.6 1.0 reshape.368
  40.0 8.0 %all-gather.1 = s32[8,1,256]{2,1,0:T(1,128)S(1)} all-gather(s32[1,1,256]{2,1,0:T(1,128)S(1)} %bitcast.115), channel_id=1, replica_groups=mesh['cp'=8,'tp'=4] {'cp'}, dimensions={0}, use_global_device_ids=true | all-gather | bytes 9216 | tf_op jit(solution)/shard_map/all_gather | solution.py:135
  48.2 0.5 multiply_cosine_fusion
  48.7 36.1 %all-gather.4.cloned.1.call-done = bf16[256,4096]{1,0:T(8,128)(2,1)} async-done(((bf16[256,1024]{1,0:T(8,128)(2,1)}), bf16[256,4096]{1,0:T(8,128)(2,1)}) %all-gather.4.cloned.1.call-update) | async-done | bytes 2097168 | tf_op jit(solution)/shard_map/all_gather | solution.py:85
  84.8 2.4 %convolution_bitcast_fusion.2 = f32[256,1,128]{0,2,1:T(8,128)S(1)} fusion(bf16[256,4096]{1,0:T(8,128)(2,1)} %all-gather.4.cloned.1.call-done, bf16[4096,128]{1,0:T(8,128)(2,1)S(1)} %copy-done), kind=kOutput, calls=%fused_computation.34 | convolution fusion | flops 268435456 | bytes 3276800 | tf_op jit(solution)/shard_map/dot_general | solution.py:87
  87.3 0.3 fusion.30
  87.6 6.3 %convolution_bitcast_fusion.1 = f32[32,8,8,128]{3,1,2,0:T(8,128)S(1)} fusion(bf16[256,4096]{1,0:T(8,128)(2,1)} %all-gather.4.cloned.1.call-done, bf16[4096,1024]{1,0:T(8,128)(2,1)} %param.10), kind=kOutput, calls=%fused_computation.33 | convolution fusion | flops 2147483648 | bytes 11534336 | tf_op jit(solution)/shard_map/dot_general | solution.py:87
  94.2 0.5 fusion.23
  94.7 0.3 maximum_bitcast_fusion
  95.0 0.9 copy.41
  95.9 10.9 %all-gather = bf16[2048,1,128]{0,2,1:T(8,128)(2,1)S(1)} all-gather(bf16[256,1,128]{0,2,1:T(8,128)(2,1)S(1)} %pad_maximum_fusion), channel_id=2, replica_groups=mesh['cp'=8,'tp'=4] {'cp'}, dimensions={0}, use_global_device_ids=true | all-gather | bytes 589824 | tf_op jit(solution)/shard_map/all_gather | solution.py:133
  106.7 0.7 convolution_convert_fusion.1
  107.4 10.0 %all_gather.15 = bf16[2048,128]{1,0:T(8,128)(2,1)S(1)} all-gather(bf16[256,128]{1,0:T(8,128)(2,1)S(1)} %convolution_convert_fusion.1), channel_id=1, replica_groups=mesh['cp'=8,'tp'=4] {'cp'}, dimensions={0}, use_global_device_ids=true | all-gather | bytes 589824 | tf_op jit(solution)/shard_map/all_gather | solution.py:134
  117.4 28.0 %while.18 = (s32[]{:T(128)}, f32[1,2048]{1,0:T(1,128)S(1)}, f32[1,2048]{1,0:T(1,128)S(1)}, f32[1,2048,128]{2,1,0:T(8,128)S(1)}, s32[256]{0:T(256)S(1)}, /*index=...) while((s32[]{:T(128)}, f32[1,2048]{1,0:T(1,128)S(1)}, ...), condition=%wide.region_8.9_spmd.clone, body=%wide.region_4.8_spmd.clone.sunk | while | flops 551702784 | bytes 22166840 | solution.py:148
  118.0 0.5 tile.22
  118.4 0.6 copy.49
  119.1 2.0 fusion.53
  121.1 1.2 fusion.55
  122.4 2.0 %fusion.57 = f32[1,2048,128]{2,1,0:T(8,128)S(1)} fusion(pred[2048,512]{0,1:T(8,128)(4,1)S(1)} %bitcast.98, f32[512,2048]{1,0:T(8,128)S(1)} %get-tuple-element.403, f32[2048]{0:T(1024)S(1)} %bitcast.102, f32[1,2048,128]{2,1,0:T(8,128)S(1)} %get-tuple-element.424, f32[2048]{0:T(1024)S(1)} %bitcast.111, pred[]{:T(512)S(6)} %compare.3, ...), kind=kOutput, calls=%fused_computation.8.clone.1 | convolution fusion | flops 274464768 | bytes 7487493 | tf_op jit(solution)/shard_map/while/body/eval_jaxpr/khs,ksd->khd/dot_general | solution.py:120
  125.0 0.5 tile.22
  125.5 0.6 copy.49
  126.1 2.0 fusion.53
  128.1 1.2 fusion.55
  129.4 2.1 %fusion.57 = f32[1,2048,128]{2,1,0:T(8,128)S(1)} fusion(pred[2048,512]{0,1:T(8,128)(4,1)S(1)} %bitcast.98, f32[512,2048]{1,0:T(8,128)S(1)} %get-tuple-element.403, f32[2048]{0:T(1024)S(1)} %bitcast.102, f32[1,2048,128]{2,1,0:T(8,128)S(1)} %get-tuple-element.424, f32[2048]{0:T(1024)S(1)} %bitcast.111, pred[]{:T(512)S(6)} %compare.3, ...), kind=kOutput, calls=%fused_computation.8.clone.1 | convolution fusion | flops 274464768 | bytes 7487493 | tf_op jit(solution)/shard_map/while/body/eval_jaxpr/khs,ksd->khd/dot_general | solution.py:120
  132.0 0.5 tile.22
  132.5 0.6 copy.49
  133.1 2.0 fusion.53
  135.1 1.2 fusion.55
  136.4 2.0 %fusion.57 = f32[1,2048,128]{2,1,0:T(8,128)S(1)} fusion(pred[2048,512]{0,1:T(8,128)(4,1)S(1)} %bitcast.98, f32[512,2048]{1,0:T(8,128)S(1)} %get-tuple-element.403, f32[2048]{0:T(1024)S(1)} %bitcast.102, f32[1,2048,128]{2,1,0:T(8,128)S(1)} %get-tuple-element.424, f32[2048]{0:T(1024)S(1)} %bitcast.111, pred[]{:T(512)S(6)} %compare.3, ...), kind=kOutput, calls=%fused_computation.8.clone.1 | convolution fusion | flops 274464768 | bytes 7487493 | tf_op jit(solution)/shard_map/while/body/eval_jaxpr/khs,ksd->khd/dot_general | solution.py:120
  139.0 0.5 tile.22
  139.5 0.6 copy.49
  140.1 2.0 fusion.53
  142.1 1.2 fusion.55
  143.4 2.1 %fusion.57 = f32[1,2048,128]{2,1,0:T(8,128)S(1)} fusion(pred[2048,512]{0,1:T(8,128)(4,1)S(1)} %bitcast.98, f32[512,2048]{1,0:T(8,128)S(1)} %get-tuple-element.403, f32[2048]{0:T(1024)S(1)} %bitcast.102, f32[1,2048,128]{2,1,0:T(8,128)S(1)} %get-tuple-element.424, f32[2048]{0:T(1024)S(1)} %bitcast.111, pred[]{:T(512)S(6)} %compare.3, ...), kind=kOutput, calls=%fused_computation.8.clone.1 | convolution fusion | flops 274464768 | bytes 7487493 | tf_op jit(solution)/shard_map/while/body/eval_jaxpr/khs,ksd->khd/dot_general | solution.py:120
  145.5 0.3 divide_convert_fusion
  145.8 0.2 copy.43
  146.1 7.1 %convolution_convert_fusion = bf16[256,4096]{1,0:T(8,128)(2,1)} fusion(bf16[256,1024]{0,1:T(8,128)(2,1)S(1)} %bitcast.103, bf16[1024,4096]{1,0:T(8,128)(2,1)} %param.13), kind=kOutput, calls=%fused_computation.32 | convolution fusion | flops 2148532224 | bytes 11010048 | tf_op jit(solution)/shard_map/dot_general | solution.py:157
  153.2 41.7 %reduce-scatter.2.cloned.1.call-done = bf16[256,1024]{1,0:T(8,128)(2,1)} async-done(((bf16[256,4096]{1,0:T(8,128)(2,1)}), bf16[256,1024]{1,0:T(8,128)(2,1)}) %reduce-scatter.2.cloned.1.call-update) | async-done | bytes 524304 | tf_op jit(solution)/shard_map/reduce_scatter | solution.py:158
  (64 shorter events, 3.7 us)
Async XLA Ops:
  6.5 78.3 %copy-start = (bf16[4096,128]{1,0:T(8,128)(2,1)S(1)}, bf16[4096,128]{1,0:T(8,128)(2,1)}, u32[]{:S(2)}) copy-start(bf16[4096,128]{1,0:T(8,128)(2,1)} %param.11) | copy-start | bytes 3145732
  9.2 14.9 %all-to-all-start = ((bf16[2,8,16384]{2,0,1:T(2,128)(2,1)}), bf16[2,8,16384]{2,0,1:T(2,128)(2,1)S(1)}, u32[]{:S(2)}, u32[]{:S(2)}) async-start(bf16[2,8,16384]{2,0,1:T(2,128)(2,1)} %copy.37), calls=%async_computation | async-start | bytes 1048576 | tf_op jit(solution)/shard_map/all_to_all | solution.py:75
  14.4 70.4 %all-gather.4.cloned.1.call-start = ((), (), s32[]{:S(2)}) async-start(), calls=%async_computation.3 | async-start | bytes 2621440 | tf_op jit(solution)/shard_map/all_gather | solution.py:85
  24.4 15.4 %copy-start.3 = (s32[9]{0:T(128)S(1)}, s32[9]{0:T(128)}, u32[]{:S(2)}) copy-start(s32[9]{0:T(128)} %param.14) | copy-start | bytes 112
  39.7 155.2 %reduce-scatter.2.cloned.1.call-start = ((), (), s32[]{:S(2)}) async-start(), calls=%async_computation.4 | async-start | bytes 2621440 | tf_op jit(solution)/shard_map/reduce_scatter | solution.py:158
  93.9 12.8 %copy-start.1 = (bf16[256,4096]{1,0:T(8,128)(2,1)S(1)}, bf16[256,4096]{1,0:T(8,128)(2,1)}, u32[]{:S(2)}) copy-start(bf16[256,4096]{1,0:T(8,128)(2,1)} %all-gather.4.cloned.1.call-done) | copy-start | bytes 6291460
  93.9 12.8 %copy-start.2 = (bf16[4096,128]{1,0:T(8,128)(2,1)S(1)}, bf16[4096,128]{1,0:T(8,128)(2,1)}, u32[]{:S(2)}) copy-start(bf16[4096,128]{1,0:T(8,128)(2,1)} %param.12) | copy-start | bytes 3145732
Sparse Core Ops, SparseCore 0:
  39.8 45.0 all-gather.3
  153.3 41.4 reduce-scatter.1
where the time goes:
time: 202 us
  waiting for transfers between devices  85.5 us (42%)
  blocking collectives  40.9 us (20%)
  matrix products  32.6 us (16%)
  between operations  13.6 us (7%)
  local copies, waits for them, and re-layouts  11.8 us (6%)
  other arithmetic  11.7 us (6%)
  starting transfers between devices  5.28 us (3%)
    reduce_scatter x1, waiting for transfers between devices, output_rows(): lax.psum_scatter(head_terms.astype(jnp.bfloat16), 'tp', scatter_dimension...  41.7 us
    all_gather x1, waiting for transfers between devices, project(): portion = lax.all_gather(local_rows, 'tp', axis=1, tiled=True)  36.1 us
    all_to_all x1, blocking collectives, relayout(): lax.all_to_all(outgoing, 'cp', split_axis=1, concat_axis=1, tiled=True)  12.1 us
    all_gather x1, blocking collectives, attend(): key_part = lax.all_gather(key_rows, 'cp', axis=0, tiled=True)  10.9 us
    all_gather x1, blocking collectives, attend(): value_part = lax.all_gather(value_rows, 'cp', axis=0, tiled=True)  9.99 us
    dot_general x3, matrix products, project(): jnp.dot(portion, weight, preferred_element_type=jnp.float32)  9.46 us
    dot_general x4, matrix products, update(): jnp.einsum('khs,ksd->khd', weights.astype(jnp.bfloat16), per_head_values,...  8.2 us
    all_gather x1, blocking collectives, attend(): token_part = lax.all_gather(key_tokens, 'cp', axis=0, tiled=True)  7.96 us
  transfers between devices with their start and end apart: 3, of which 3 were waited for; matrix products, arithmetic and copies ran while one was open for 1% of the time, Pallas kernels for 0%

commit v1 on v0

--- a/solution.py
+++ b/solution.py
@@ -72,7 +72,9 @@
     per_device = row_count // BLOCK
     portion = BLOCK // cp_size
     pieces = local_rows.reshape(per_device, cp_size, portion * row_width)
-    spread = lax.all_to_all(pieces, "cp", split_axis=1, concat_axis=0, tiled=True)
+    parts = jnp.split(pieces, lax.axis_size("cp"), axis=1)
+    incoming = lax.all_to_all(jnp.stack(parts), "cp", 0, 0)
+    spread = jnp.concatenate(incoming, axis=0)
     spread = spread.reshape(per_device * cp_size, portion * row_width)
     wanted = block_order.reshape(cp_size, per_device).T.reshape(-1)
     outgoing = jnp.take(spread, wanted, axis=0).reshape(per_device, cp_size, portion * row_width)

time: 202 us -> 208 us (1.030)
  local copies, waits for them, and re-layouts: 11.8 us -> 17.5 us
    unnamed x9 -> x18, local copies, waits for them, and re-layouts: 0.22 us -> 5.35 us
where the time goes in v1:
time: 208 us; the launch traced here: 207 us
  waiting for transfers between devices  86.8 us (42%)
  blocking collectives  40.9 us (20%)
  matrix products  32.6 us (16%)
  local copies, waits for them, and re-layouts  17.5 us (8%)
  between operations  13.6 us (7%)
  other arithmetic  10.3 us (5%)
  starting transfers between devices  5.28 us (3%)
    reduce_scatter x1, waiting for transfers between devices, output_rows(): lax.psum_scatter(head_terms.astype(jnp.bfloat16), 'tp', scatter_dimension...  41.7 us
    all_gather x1, waiting for transfers between devices, project(): portion = lax.all_gather(local_rows, 'tp', axis=1, tiled=True)  36.1 us
    all_to_all x1, blocking collectives, relayout(): lax.all_to_all(outgoing, 'cp', split_axis=1, concat_axis=1, tiled=True)  12.1 us
    all_gather x1, blocking collectives, attend(): key_part = lax.all_gather(key_rows, 'cp', axis=0, tiled=True)  10.9 us
    all_gather x1, blocking collectives, attend(): value_part = lax.all_gather(value_rows, 'cp', axis=0, tiled=True)  9.99 us
    dot_general x3, matrix products, project(): jnp.dot(portion, weight, preferred_element_type=jnp.float32)  9.45 us
    all_to_all x1, waiting for transfers between devices, relayout(): incoming = lax.all_to_all(jnp.stack(parts), 'cp', 0, 0)  9.06 us
    dot_general x4, matrix products, update(): jnp.einsum('khs,ksd->khd', weights.astype(jnp.bfloat16), per_head_values,...  8.2 us
  transfers between devices with their start and end apart: 3, of which 3 were waited for; matrix products, arithmetic and copies ran while one was open for 1% of the time, Pallas kernels for 0%

profile of v1, /device:TPU:0, one launch (start us, length us, event | category | flops | bytes accessed | tf_op | source)
XLA Modules:
  0.0 207.4 jit_solution(3317377636567359963)
XLA Ops:
  6.5 1.4 reshape.361
  7.9 1.1 fusion.36
  9.1 0.7 bitcast_dynamic-update-slice_fusion.7
  9.8 0.7 bitcast_dynamic-update-slice_fusion.6
  10.5 0.7 bitcast_dynamic-update-slice_fusion.5
  11.3 0.7 bitcast_dynamic-update-slice_fusion.4
  12.0 0.7 bitcast_dynamic-update-slice_fusion.3
  12.7 0.7 bitcast_dynamic-update-slice_fusion.2
  13.5 0.7 bitcast_dynamic-update-slice_fusion.1
  14.2 0.7 bitcast_dynamic-update-slice_fusion
  14.9 5.2 %all-to-all-start = ((bf16[8,2,1,16384]{3,1,2,0:T(2,128)(2,1)}), bf16[8,2,1,16384]{3,1,2,0:T(2,128)(2,1)S(1)}, u32[]{:S(2)}, u32[]{:S(2)}) async-start(bf16[8,2,1,16384]{3,1,2,0:T(2,128)(2,1)} %bitcast_dynamic-update-slice_fusion), calls=%async_computation | async-start | bytes 1048576 | tf_op jit(solution)/shard_map/all_to_all | solution.py:76
  20.8 9.1 %all-to-all-done = bf16[8,2,1,16384]{3,1,2,0:T(2,128)(2,1)S(1)} async-done(((bf16[8,2,1,16384]{3,1,2,0:T(2,128)(2,1)}), bf16[8,2,1,16384]{3,1,2,0:T(2,128)(2,1)S(1)}, u32[]{:S(2)}, u32[]{:S(2)}) %all-to-all-start) | async-done | bytes 524320 | tf_op jit(solution)/shard_map/all_to_all | solution.py:76
  30.0 0.9 gather_fusion
  30.9 0.9 broadcast_select_fusion.2
  31.8 12.1 %all_to_all.10 = bf16[2,8,16384]{2,0,1:T(2,128)(2,1)S(1)} all-to-all(bf16[2,8,16384]{2,0,1:T(2,128)(2,1)S(1)} %broadcast_select_fusion.2), channel_id=1, replica_groups=mesh['cp'=8,'tp'=4] {'cp'}, dimensions={1} | all-to-all | bytes 1048576 | tf_op jit(solution)/shard_map/all_to_all | solution.py:81
  44.3 1.0 reshape.363
  45.6 8.0 %all-gather.1 = s32[8,1,256]{2,1,0:T(1,128)S(1)} all-gather(s32[1,1,256]{2,1,0:T(1,128)S(1)} %bitcast.127), channel_id=1, replica_groups=mesh['cp'=8,'tp'=4] {'cp'}, dimensions={0}, use_global_device_ids=true | all-gather | bytes 9216 | tf_op jit(solution)/shard_map/all_gather | solution.py:137
  53.9 0.5 multiply_cosine_fusion
  54.4 36.1 %all-gather.4.cloned.1.call-done = bf16[256,4096]{1,0:T(8,128)(2,1)} async-done(((bf16[256,1024]{1,0:T(8,128)(2,1)}), bf16[256,4096]{1,0:T(8,128)(2,1)}) %all-gather.4.cloned.1.call-update) | async-done | bytes 2097168 | tf_op jit(solution)/shard_map/all_gather | solution.py:87
  90.5 2.4 %convolution_bitcast_fusion.2 = f32[256,1,128]{0,2,1:T(8,128)S(1)} fusion(bf16[256,4096]{1,0:T(8,128)(2,1)} %all-gather.4.cloned.1.call-done, bf16[4096,128]{1,0:T(8,128)(2,1)S(1)} %copy-done), kind=kOutput, calls=%fused_computation.34 | convolution fusion | flops 268435456 | bytes 3276800 | tf_op jit(solution)/shard_map/dot_general | solution.py:89
  93.3 6.3 %convolution_bitcast_fusion.1 = f32[32,8,8,128]{3,1,2,0:T(8,128)S(1)} fusion(bf16[256,4096]{1,0:T(8,128)(2,1)} %all-gather.4.cloned.1.call-done, bf16[4096,1024]{1,0:T(8,128)(2,1)} %param.10), kind=kOutput, calls=%fused_computation.33 | convolution fusion | flops 2147483648 | bytes 11534336 | tf_op jit(solution)/shard_map/dot_general | solution.py:89
  99.8 0.5 fusion.23
  100.7 0.9 copy.135
  101.5 10.9 %all-gather = bf16[2048,1,128]{0,2,1:T(8,128)(2,1)S(1)} all-gather(bf16[256,1,128]{0,2,1:T(8,128)(2,1)S(1)} %pad_maximum_fusion), channel_id=2, replica_groups=mesh['cp'=8,'tp'=4] {'cp'}, dimensions={0}, use_global_device_ids=true | all-gather | bytes 589824 | tf_op jit(solution)/shard_map/all_gather | solution.py:135
  112.4 0.7 convolution_convert_fusion.1
  113.1 10.0 %all_gather.15 = bf16[2048,128]{1,0:T(8,128)(2,1)S(1)} all-gather(bf16[256,128]{1,0:T(8,128)(2,1)S(1)} %convolution_convert_fusion.1), channel_id=1, replica_groups=mesh['cp'=8,'tp'=4] {'cp'}, dimensions={0}, use_global_device_ids=true | all-gather | bytes 589824 | tf_op jit(solution)/shard_map/all_gather | solution.py:136
  123.1 28.0 %while.18 = (s32[]{:T(128)}, f32[1,2048]{1,0:T(1,128)S(1)}, f32[1,2048]{1,0:T(1,128)S(1)}, f32[1,2048,128]{2,1,0:T(8,128)S(1)}, s32[256]{0:T(256)S(1)}, /*index=...) while((s32[]{:T(128)}, f32[1,2048]{1,0:T(1,128)S(1)}, ...), condition=%wide.region_8.9_spmd.clone, body=%wide.region_4.8_spmd.clone.sunk | while | flops 551702784 | bytes 22166840 | solution.py:150
  123.6 0.5 tile.22
  124.1 0.6 copy.159
  124.8 2.0 fusion.54
  126.7 1.2 fusion.56
  128.0 2.0 fusion.58
  130.6 0.5 tile.22
  131.1 0.6 copy.159
  131.8 2.0 fusion.54
  133.8 1.2 fusion.56
  135.0 2.1 fusion.58
  137.7 0.5 tile.22
  138.1 0.6 copy.159
  138.8 2.0 fusion.54
  140.8 1.2 fusion.56
  142.1 2.0 fusion.58
  145.2 0.6 copy.159
  145.8 2.0 fusion.54
  147.8 1.2 fusion.56
  149.1 2.1 fusion.58
  151.7 7.1 %convolution_convert_fusion = bf16[256,4096]{1,0:T(8,128)(2,1)} fusion(bf16[256,1024]{0,1:T(8,128)(2,1)S(1)} %bitcast.116, bf16[1024,4096]{1,0:T(8,128)(2,1)} %param.13), kind=kOutput, calls=%fused_computation.32 | convolution fusion | flops 2148532224 | bytes 11010048 | tf_op jit(solution)/shard_map/dot_general | solution.py:159
  158.9 41.7 %reduce-scatter.2.cloned.1.call-done = bf16[256,1024]{1,0:T(8,128)(2,1)} async-done(((bf16[256,4096]{1,0:T(8,128)(2,1)}), bf16[256,1024]{1,0:T(8,128)(2,1)}) %reduce-scatter.2.cloned.1.call-update) | async-done | bytes 524304 | tf_op jit(solution)/shard_map/reduce_scatter | solution.py:160
  (74 shorter events, 5.8 us)
Async XLA Ops:
  6.5 84.0 %copy-start = (bf16[4096,128]{1,0:T(8,128)(2,1)S(1)}, bf16[4096,128]{1,0:T(8,128)(2,1)}, u32[]{:S(2)}) copy-start(bf16[4096,128]{1,0:T(8,128)(2,1)} %param.11) | copy-start | bytes 3145732
  6.5 13.6 %copy-start.4 = (s32[16]{0:T(128)S(1)}, s32[16]{0:T(128)}, u32[]{:S(2)}) copy-start(s32[16]{0:T(128)} %param.15) | copy-start | bytes 196
  14.9 14.9 %all-to-all-start = ((bf16[8,2,1,16384]{3,1,2,0:T(2,128)(2,1)}), bf16[8,2,1,16384]{3,1,2,0:T(2,128)(2,1)S(1)}, u32[]{:S(2)}, u32[]{:S(2)}) async-start(bf16[8,2,1,16384]{3,1,2,0:T(2,128)(2,1)} %bitcast_dynamic-update-slice_fusion), calls=%async_computation | async-start | bytes 1048576 | tf_op jit(solution)/shard_map/all_to_all | solution.py:76
  20.1 70.4 %all-gather.4.cloned.1.call-start = ((), (), s32[]{:S(2)}) async-start(), calls=%async_computation.3 | async-start | bytes 2621440 | tf_op jit(solution)/shard_map/all_gather | solution.py:87
  30.0 15.4 %copy-start.3 = (s32[9]{0:T(128)S(1)}, s32[9]{0:T(128)}, u32[]{:S(2)}) copy-start(s32[9]{0:T(128)} %param.14) | copy-start | bytes 112
  45.3 155.2 %reduce-scatter.2.cloned.1.call-start = ((), (), s32[]{:S(2)}) async-start(), calls=%async_computation.4 | async-start | bytes 2621440 | tf_op jit(solution)/shard_map/reduce_scatter | solution.py:160
  99.6 12.8 %copy-start.1 = (bf16[256,4096]{1,0:T(8,128)(2,1)S(1)}, bf16[256,4096]{1,0:T(8,128)(2,1)}, u32[]{:S(2)}) copy-start(bf16[256,4096]{1,0:T(8,128)(2,1)} %all-gather.4.cloned.1.call-done) | copy-start | bytes 6291460
  99.6 12.8 %copy-start.2 = (bf16[4096,128]{1,0:T(8,128)(2,1)S(1)}, bf16[4096,128]{1,0:T(8,128)(2,1)}, u32[]{:S(2)}) copy-start(bf16[4096,128]{1,0:T(8,128)(2,1)} %param.12) | copy-start | bytes 3145732
Sparse Core Ops, SparseCore 0:
  45.4 45.0 all-gather.3
  159.0 41.4 reduce-scatter.1
